TPU v7x, 64 devices: a 2x2x8 block of a 4x4x8 slice. The times are simulated.
64 devices in a mesh: dp: 4 (over x, y), ep: 16 (over z, core).
Axes of the slice: x: 2, y: 2, z: 8, core: 2. Of those that a mesh axis runs over, the one named last changes fastest.
The devices are a block of a 4x4x8 slice.
Arguments:
- x: bfloat16 [4, 16, 256, 1792], P('dp', 'ep'), parts along dimension 0
- expert: int32 [4, 16, 256, 2], P('dp', 'ep'), parts along dimension 0
- slot: int32 [4, 16, 256, 2], P('dp', 'ep'), parts along dimension 0
- gate: float32 [4, 16, 256, 2], P('dp', 'ep'), parts along dimension 0
- w_gate: bfloat16 [32, 1792, 4864], P('ep')
- w_up: bfloat16 [32, 1792, 4864], P('ep')
- w_down: bfloat16 [32, 4864, 1792], P('ep')
Outputs:
- y: bfloat16 [4, 16, 256, 1792], P('dp', 'ep'), parts along dimension 0
There are 4 independent parts. A program takes and returns all parts, laid end to end along the dimension named above; an argument that names none is the same for every part.
All inputs are finite; a program needn't handle non-finite values.
Results may differ from a plain program's by a relative error of at most 0.009.
Values are sent between devices in bfloat16 or wider.
A program may use at most 768 MiB of HBM per device.

v0:
```python
import jax
import jax.numpy as jnp
from jax import lax
from jax.sharding import NamedSharding, PartitionSpec as P


def einsum(form, a, b):
    return jnp.einsum(form, a.astype(jnp.float32), b.astype(jnp.float32))


def solution(mesh):
    def placed(v, *spec):
        return lax.with_sharding_constraint(v, NamedSharding(mesh, P(*spec)))

    def step(x, expert, slot, gate, w_gate, w_up, w_down):
        experts, (tokens, top) = w_gate.shape[0], expert.shape[2:]
        slots = 5 * tokens * top // (4 * experts)
        to_expert = jax.nn.one_hot(expert, experts, dtype=jnp.bfloat16)
        to_slot = jax.nn.one_hot(slot, slots, dtype=jnp.bfloat16)
        weighted = to_expert * gate[..., None].astype(jnp.bfloat16)
        dispatch = einsum("abtke,abtkc->abtec", to_expert, to_slot).astype(jnp.bfloat16)
        combine = einsum("abtke,abtkc->abtec", weighted, to_slot).astype(jnp.bfloat16)
        z = einsum("abtec,abtd->aebcd", dispatch, x).astype(jnp.bfloat16)
        z = placed(z, "dp", None, "ep", None, None)
        z = placed(z, "dp", "ep", None, None, None)
        h = jax.nn.silu(einsum("aebcd,edf->aebcf", z, w_gate))
        h = (h * einsum("aebcd,edf->aebcf", z, w_up)).astype(jnp.bfloat16)
        out = einsum("aebcf,efd->aebcd", h, w_down).astype(jnp.bfloat16)
        out = placed(out, "dp", "ep", None, None, None)
        out = placed(out, "dp", None, "ep", None, None)
        y = einsum("abtec,aebcd->abtd", combine, out)
        return y.astype(jnp.bfloat16)

    return step
```

profile of v0, /device:TPU:21, one launch (start us, length us, event | category | flops | bytes accessed | tf_op | source)
XLA Modules:
  0.0 225.3 jit_solution(9774576442797589048)
XLA Ops:
  0.0 0.0 copy-start
  0.0 0.9 copy.11
  0.9 0.0 copy-start.2
  0.9 0.8 copy.9
  1.8 0.0 copy-done.2
  1.8 0.0 copy-start.4
  1.8 0.7 copy-done.4
  2.4 2.8 %convolution_convert_fusion.1 = bf16[256,32,20]{1,2,0:T(8,128)(2,1)S(1)} fusion(s32[256,2]{1,0:T(8,128)S(1)} %copy.11, s32[256,2]{1,0:T(8,128)S(1)} %copy.9), kind=kOutput, calls=%fused_computation.25 | convolution fusion | flops 845824 | bytes 331776 | tf_op jit(solution)/abtke,abtkc->abtec/dot_general | solution.py:8
  5.2 0.0 copy-done
  5.2 1.1 convolution_convert_fusion
  6.3 2.3 %reshape.6 = bf16[1,16,2,1,20,1792]{5,2,1,4,3,0:T(2,128)(2,1)} reshape(bf16[32,20,1792]{2,0,1:T(8,128)(2,1)S(1)} %convolution_convert_fusion) | data formatting | bytes 4587520 | tf_op jit(solution)/sharding_constraint;jit(solution)/sharding_constraint | solution.py:13
  8.6 3.2 %copy.13 = bf16[1,16,2,1,20,1792]{5,2,4,3,0,1:T(2,128)(2,1)S(1)} copy(bf16[1,16,2,1,20,1792]{5,2,1,4,3,0:T(2,128)(2,1)} %reshape.6) | data formatting | bytes 4587520 | tf_op jit(solution)/sharding_constraint;jit(solution)/sharding_constraint | solution.py:13
  11.9 65.5 %all-to-all.4 = bf16[1,16,2,1,20,1792]{5,2,4,3,0,1:T(2,128)(2,1)S(1)} all-to-all(bf16[1,16,2,1,20,1792]{5,2,4,3,0,1:T(2,128)(2,1)S(1)} %copy.13), channel_id=1, replica_groups=mesh['dp'=4,'ep'=16] {'ep'}, dimensions={1} | all-to-all | bytes 4587520 | tf_op jit(solution)/sharding_constraint;jit(solution)/sharding_constraint | solution.py:13
  77.3 23.1 %fusion.4 = f32[2,16,20,4864]{3,2,1,0:T(8,128)} fusion(bf16[2,1792,4864]{2,1,0:T(8,128)(2,1)} %param.4, bf16[1,16,2,1,20,1792]{5,2,4,3,0,1:T(2,128)(2,1)S(1)} %all-to-all.4), kind=kOutput, calls=%fused_computation.4 | convolution fusion | flops 11156848640 | bytes 49610752 | tf_op jit(solution)/aebcd,edf->aebcf/dot_general | solution.py:8
  100.4 27.6 %fusion.12.clone.8 = bf16[2,16,20,4864]{3,2,1,0:T(8,128)(2,1)} fusion(bf16[2,1792,4864]{2,1,0:T(8,128)(2,1)} %param.5, f32[2,16,20,4864]{3,2,1,0:T(8,128)} %fusion.4, bf16[1,16,2,1,20,1792]{5,2,4,3,0,1:T(2,128)(2,1)S(1)} %all-to-all.4), kind=kOutput, calls=%fused_computation.13.clone.clone.clone.clone.clone.clone.clone.1 | convolution fusion | flops 11175526400 | bytes 55836672 | tf_op jit(solution)/aebcd,edf->aebcf/dot_general | solution.py:8
  128.0 22.1 %fusion.23 = bf16[1,2,16,1,20,1792]{5,4,2,1,3,0:T(8,128)(2,1)} fusion(bf16[2,4864,1792]{2,1,0:T(8,128)(2,1)} %param.6, bf16[2,16,20,4864]{3,2,1,0:T(8,128)(2,1)} %fusion.12.clone.8), kind=kOutput, calls=%fused_computation.17 | convolution fusion | flops 11157995520 | bytes 43384832 | tf_op jit(solution)/aebcf,efd->aebcd/dot_general | solution.py:8
  150.1 5.6 %copy.15 = bf16[1,2,16,1,20,1792]{5,1,4,3,0,2:T(2,128)(2,1)} copy(bf16[1,2,16,1,20,1792]{5,4,2,1,3,0:T(8,128)(2,1)} %fusion.23) | data formatting | bytes 4587520 | tf_op jit(solution)/sharding_constraint;jit(solution)/sharding_constraint | solution.py:13
  155.6 0.0 copy-start.6
  155.6 0.0 copy-start.3
  155.6 0.0 copy-start.5
  155.6 4.3 %all-to-all-start.1 = ((bf16[1,2,16,1,20,1792]{5,1,4,3,0,2:T(2,128)(2,1)}), bf16[1,2,16,1,20,1792]{5,1,4,3,0,2:T(2,128)(2,1)S(1)}, u32[]{:S(2)}, u32[]{:S(2)}) async-start(bf16[1,2,16,1,20,1792]{5,1,4,3,0,2:T(2,128)(2,1)} %copy.15), calls=%async_computation.1 | async-start | bytes 4587520 | tf_op jit(solution)/sharding_constraint;jit(solution)/sharding_constraint | solution.py:13
  159.9 0.0 copy-done.6
  160.0 0.1 copy.10
  160.1 0.0 copy-done.3
  160.1 0.0 copy-done.5
  160.1 3.9 %convolution_convert_fusion.2 = bf16[256,32,20]{1,2,0:T(8,128)(2,1)} fusion(s32[256,2]{1,0:T(8,128)S(1)} %copy-done.3, s32[256,2]{1,0:T(8,128)S(1)} %copy-done.5, bf16[256,2]{1,0:T(8,128)(2,1)S(1)} %copy.10), kind=kOutput, calls=%fused_computation.26 | convolution fusion | flops 862208 | bytes 332800 | tf_op jit(solution)/abtke,abtkc->abtec/dot_general | solution.py:8
  164.0 49.1 %all-to-all-done.1 = bf16[1,2,16,1,20,1792]{5,1,4,3,0,2:T(2,128)(2,1)S(1)} async-done(((bf16[1,2,16,1,20,1792]{5,1,4,3,0,2:T(2,128)(2,1)}), bf16[1,2,16,1,20,1792]{5,1,4,3,0,2:T(2,128)(2,1)S(1)}, u32[]{:S(2)}, u32[]{:S(2)}) %all-to-all-start.1) | async-done | bytes 2293792 | tf_op jit(solution)/sharding_constraint;jit(solution)/sharding_constraint | solution.py:13
  213.1 3.7 %copy.16 = bf16[1,16,2,1,20,1792]{5,2,1,4,3,0:T(2,128)(2,1)} copy(bf16[1,16,2,1,20,1792]{5,2,4,3,0,1:T(2,128)(2,1)S(1)} %bitcast.132) | data formatting | bytes 4587520 | tf_op jit(solution)/sharding_constraint;jit(solution)/sharding_constraint | solution.py:13
  216.8 4.8 %reshape.46 = bf16[32,20,1792]{2,0,1:T(8,128)(2,1)S(1)} reshape(bf16[1,16,2,1,20,1792]{5,2,1,4,3,0:T(2,128)(2,1)} %copy.16) | data formatting | bytes 4587520
  221.6 0.0 copy-start.1
  221.7 3.6 %fusion.35 = bf16[1,1,256,1792]{3,2,1,0:T(8,128)(2,1)} fusion(bf16[32,20,1792]{2,0,1:T(8,128)(2,1)S(1)} %reshape.46, bf16[256,32,20]{1,2,0:T(8,128)(2,1)} %convolution_convert_fusion.2), kind=kOutput, calls=%fused_computation.24 | convolution fusion | flops 587661312 | bytes 3538944 | tf_op jit(solution)/abtec,aebcd->abtd/dot_general | solution.py:8
  225.3 0.0 copy-done.1
  (1 shorter events, 0.0 us)
Async XLA Ops:
  0.0 5.2 %copy-start = (bf16[1,1,256,1792]{3,2,1,0:T(8,128)(2,1)S(1)}, bf16[1,1,256,1792]{3,2,1,0:T(8,128)(2,1)}, u32[]{:S(2)}) copy-start(bf16[1,1,256,1792]{3,2,1,0:T(8,128)(2,1)} %param.3) | copy-start | bytes 2752516
  0.9 0.9 copy-start.2
  1.8 0.7 copy-start.4
  155.6 4.3 %copy-start.6 = (f32[1,1,256,2]{2,3,1,0:T(2,128)S(1)}, f32[1,1,256,2]{2,3,1,0:T(2,128)}, u32[]{:S(2)}) copy-start(f32[1,1,256,2]{2,3,1,0:T(2,128)} %param.1) | copy-start | bytes 6148
  155.6 4.5 %copy-start.3 = (s32[256,2]{1,0:T(8,128)S(1)}, s32[256,2]{1,0:T(8,128)}, u32[]{:S(2)}) copy-start(s32[256,2]{1,0:T(8,128)} %copy-done.2) | copy-start | bytes 6148
  155.6 4.5 %copy-start.5 = (s32[256,2]{1,0:T(8,128)S(1)}, s32[256,2]{1,0:T(8,128)}, u32[]{:S(2)}) copy-start(s32[256,2]{1,0:T(8,128)} %copy-done.4) | copy-start | bytes 6148
  155.6 57.4 %all-to-all-start.1 = ((bf16[1,2,16,1,20,1792]{5,1,4,3,0,2:T(2,128)(2,1)}), bf16[1,2,16,1,20,1792]{5,1,4,3,0,2:T(2,128)(2,1)S(1)}, u32[]{:S(2)}, u32[]{:S(2)}) async-start(bf16[1,2,16,1,20,1792]{5,1,4,3,0,2:T(2,128)(2,1)} %copy.15), calls=%async_computation.1 | async-start | bytes 4587520 | tf_op jit(solution)/sharding_constraint;jit(solution)/sharding_constraint | solution.py:13
  221.6 3.7 %copy-start.1 = (bf16[1,1,256,1792]{3,2,1,0:T(8,128)(2,1)S(1)}, bf16[1,1,256,1792]{3,2,1,0:T(8,128)(2,1)}, u32[]{:S(2)}) copy-start(bf16[1,1,256,1792]{3,2,1,0:T(8,128)(2,1)} %param.3) | copy-start | bytes 2752516
where the time goes:
time: 226 us; the launch traced here: 225 us
  matrix products  84.2 us (37%)
  blocking collectives  65.5 us (29%)
  waiting for transfers between devices  49.1 us (22%)
  local copies, waits for them, and re-layouts  22.2 us (10%)
  starting transfers between devices  4.28 us (2%)
    dot_general x7, matrix products, einsum(): return jnp.einsum(form, a.astype(jnp.float32), b.astype(jnp.float32))  84.2 us
    another operation x1, blocking collectives, placed(): return lax.with_sharding_constraint(v, NamedSharding(mesh, P(*spec)))  65.5 us
    another operation x1, waiting for transfers between devices, placed(): return lax.with_sharding_constraint(v, NamedSharding(mesh, P(*spec)))  49.1 us
    another operation x4, local copies, waits for them, and re-layouts, placed(): return lax.with_sharding_constraint(v, NamedSharding(mesh, P(*spec)))  14.8 us
    unnamed x17, local copies, waits for them, and re-layouts  7.26 us
  transfers between devices with their start and end apart: 1, of which 1 were waited for; matrix products, arithmetic and copies ran while one was open for 2% of the time, Pallas kernels for 0%

commit v1 on v0

v1 whole, which is shorter than its diff:
```python
import functools

import jax
import jax.numpy as jnp
from jax import lax
from jax.experimental import pallas as pl
from jax.experimental.pallas import tpu as pltpu
from jax.sharding import PartitionSpec as P

CORES = 2
TILE = 256
RING = 16
GROUP = 4
FAR = 1 << 16


def dot(a, b):
    return jnp.dot(a, b, preferred_element_type=jnp.float32)


def offsets(n):
    chips = n // CORES
    out = []
    for far in range(chips // 2, 0, -1):
        for way in (1, -1):
            if way == -1 and 2 * far == chips:
                continue
            for core in range(CORES):
                out.append(((way * far) % chips, core))
    return out + [(0, core) for core in range(CORES - 1, -1, -1)]


def kernel(n, slots, experts, flat_ref, gate_ref, x_hbm, wg_hbm, wu_hbm, wd_hbm, y_ref,
           xs, zsend, zrecv, osend, orecv, z, acc, yacc, hid, cols, gcols, wg, wu, wd,
           xsem, wsem, ssem, rsem):
    plan = offsets(n)
    self_at = n - 1
    chips = n // CORES
    me = lax.axis_index("ep")
    chip, core = me // CORES, lax.rem(me, CORES)
    dim = x_hbm.shape[1]
    half = dim // 2
    tokens = x_hbm.shape[0]
    rows = 2 * slots
    tiles = wd_hbm.shape[1] // TILE
    total = experts * tiles
    ring = wg.shape[0]

    def partner(i, back):
        ahead, other = plan[i]
        ahead = (chips - ahead) % chips if back else ahead
        return lax.rem(chip + ahead, chips) * CORES + lax.rem(core + other, CORES)

    def weight_copy(q, which):
        e, f = q // tiles, lax.rem(q, tiles)
        slot = lax.rem(q, ring)
        at = pl.ds(pl.multiple_of(f * TILE, TILE), TILE)
        if which == 2:
            return pltpu.make_async_copy(wd_hbm.at[e, at, :], wd.at[slot], wsem.at[2, slot])
        src, dst = ((wg_hbm, wg), (wu_hbm, wu))[which]
        return pltpu.make_async_copy(src.at[e, :, at], dst.at[slot], wsem.at[which, slot])

    def remote(phase, e, i, src, dst, back):
        return pltpu.make_async_remote_copy(
            src_ref=src.at[e, i], dst_ref=dst.at[e, i],
            send_sem=ssem.at[phase, i], recv_sem=rsem.at[phase, i],
            device_id={"ep": partner(i, back)}, device_id_type=pl.DeviceIdType.MESH)

    out_copy = lambda e, i: remote(e, e, i, zsend, zrecv, False)
    back_copy = lambda e, i: remote(experts + e, e, i, osend, orecv, True)

    xcopies = [pltpu.make_async_copy(x_hbm.at[:, pl.ds(k * half, half)], xs.at[pl.ds(k * tokens, tokens), :], xsem.at[k])
               for k in range(2)]
    for c in xcopies:
        c.start()

    barrier = pltpu.get_barrier_semaphore()
    for k in range(1, n):
        pl.semaphore_signal(barrier, inc=1, device_id={"ep": lax.rem(me + k, n)}, device_id_type=pl.DeviceIdType.MESH)

    @pl.loop(0, ring)
    def _(q):
        for which in range(3):
            weight_copy(q, which).start()

    def wanted(e, g, shape, axis):
        at = lax.broadcasted_iota(jnp.int32, shape, axis)
        want = jnp.zeros(shape, jnp.int32)
        for j in range(GROUP):
            inside = at - j * rows
            first = partner(g * GROUP + j, False) * (experts * slots) + e * slots
            value = first + inside + jnp.where(inside >= slots, FAR - slots, 0)
            want = jnp.where(inside >= 0, value, want)
        return want

    def dispatch(e, g):
        want = wanted(e, g, (GROUP * rows, 2 * tokens), 0)
        hit = (flat_ref[0:1, :] == want) | (flat_ref[1:2, :] == want)
        mask = jnp.where(hit, 1.0, 0.0).astype(jnp.bfloat16)
        packed = dot(mask, xs[...]).astype(jnp.bfloat16)
        for j in range(GROUP):
            i = g * GROUP + j
            piece = packed[j * rows:(j + 1) * rows]
            if i == self_at:
                zrecv[e, i] = piece
            else:
                zsend[e, i] = piece

    groups = n // GROUP
    for c in xcopies:
        c.wait()
    for g in range(groups):
        dispatch(0, g)
    pl.semaphore_wait(barrier, n - 1)
    for i in range(self_at):
        out_copy(0, i).start()
    for g in range(groups):
        dispatch(1, g)
    for k in range(2):
        cols[k] = jnp.broadcast_to(flat_ref[k:k + 1, :], (128, 2 * tokens)).T
        rounded = gate_ref[k:k + 1, :].astype(jnp.bfloat16).astype(jnp.float32)
        gcols[k] = jnp.broadcast_to(rounded, (128, 2 * tokens)).T
    for i in range(self_at):
        out_copy(0, i).wait_send()
        out_copy(1, i).start()

    quarter = GROUP * slots

    def spread(shape, axis, second):
        r = lax.broadcasted_iota(jnp.int32, shape, axis)
        step = jnp.zeros(shape, jnp.int32)
        for j in range(1, GROUP):
            step = step + jnp.where(r >= j * slots, slots, 0)
        return r + step + (slots if second else 0)

    def gather(e):
        shape = (quarter, GROUP * rows)
        there = lax.broadcasted_iota(jnp.int32, shape, 1)
        for g in range(groups):
            for j in range(GROUP):
                i = g * GROUP + j
                if i != self_at:
                    out_copy(e, i).wait_recv()
            got = zrecv[e, g * GROUP:(g + 1) * GROUP].reshape(GROUP * rows, half)
            for k in range(2):
                pick = jnp.where(there == spread(shape, 0, k == 1), 1.0, 0.0).astype(jnp.bfloat16)
                z[g * quarter:(g + 1) * quarter, k * half:(k + 1) * half] = dot(pick, got).astype(jnp.bfloat16)

    def up(q):
        slot = lax.rem(q, ring)
        weight_copy(q, 0).wait()
        weight_copy(q, 1).wait()
        a = dot(z[...], wg[slot])
        b = dot(z[...], wu[slot])
        return (jax.nn.silu(a) * b).astype(jnp.bfloat16)

    def refill(q, which):
        @pl.when(q + ring < total)
        def _():
            weight_copy(q + ring, which).start()

    def expert(e):
        base = e * tiles
        hid[0] = up(base)
        refill(base, 0)
        refill(base, 1)
        acc[...] = jnp.zeros_like(acc)

        def step(f, _):
            q = base + f
            weight_copy(q - 1, 2).wait()
            old = hid[lax.rem(f + 1, 2)]
            new = up(q)
            acc[...] += dot(old, wd[lax.rem(q - 1, ring)])
            hid[lax.rem(f, 2)] = new
            refill(q, 0)
            refill(q, 1)
            refill(q - 1, 2)
            return 0

        lax.fori_loop(1, tiles, step, 0)
        last = base + tiles - 1
        weight_copy(last, 2).wait()
        acc[...] += dot(hid[(tiles - 1) % 2], wd[last % ring])
        refill(last, 2)

    def give_back(e):
        shape = (GROUP * rows, quarter)
        there = lax.broadcasted_iota(jnp.int32, shape, 0)
        for g in range(groups):
            done = acc[g * quarter:(g + 1) * quarter, :].astype(jnp.bfloat16)
            packed = jnp.zeros((GROUP * rows, half), jnp.float32)
            for k in range(2):
                pick = jnp.where(there == spread(shape, 1, k == 1), 1.0, 0.0).astype(jnp.bfloat16)
                packed += dot(pick, done[:, k * half:(k + 1) * half])
            packed = packed.astype(jnp.bfloat16)
            for j in range(GROUP):
                i = g * GROUP + j
                piece = packed[j * rows:(j + 1) * rows]
                if i == self_at:
                    orecv[e, i] = piece
                else:
                    osend[e, i] = piece
            for j in range(GROUP):
                i = g * GROUP + j
                if i != self_at:
                    back_copy(e, i).start()

    def combine(e):
        shape = (2 * tokens, GROUP * rows)
        for g in range(groups):
            want = wanted(e, g, shape, 1)
            weight = jnp.zeros(shape, jnp.float32)
            for k in range(2):
                weight += jnp.where(cols[k, :, 0:1] == want, gcols[k, :, 0:1], 0.0)
            weight = weight.astype(jnp.bfloat16)
            for j in range(GROUP):
                i = g * GROUP + j
                if i != self_at:
                    back_copy(e, i).wait_recv()
            term = dot(weight, orecv[e, g * GROUP:(g + 1) * GROUP].reshape(GROUP * rows, half))
            if e == 0 and g == 0:
                yacc[...] = term
            else:
                yacc[...] += term

    for e in range(experts):
        gather(e)
        expert(e)
        give_back(e)
    for e in range(experts):
        combine(e)
    for k in range(2):
        y_ref[:, k * half:(k + 1) * half] = yacc[k * tokens:(k + 1) * tokens, :].astype(jnp.bfloat16)
    for i in range(self_at):
        out_copy(1, i).wait_send()
        for e in range(experts):
            back_copy(e, i).wait_send()


def solution(mesh):
    n = mesh.shape["ep"]

    def step(x, expert, slot, gate, w_gate, w_up, w_down):
        tokens, dim = x.shape[2:]
        top = expert.shape[3]
        experts, _, ff = w_gate.shape
        slots = 5 * tokens * top // (4 * experts * n)
        rows, half = 2 * slots, dim // 2
        expert, slot, gate = (v.reshape(tokens, top).T for v in (expert, slot, gate))
        flat = jnp.where(slot < slots, expert * slots + slot, -1)
        flat = jnp.concatenate([flat, flat + FAR], axis=1)
        gate = jnp.concatenate([gate, gate], axis=1)
        vmem = pl.BlockSpec(memory_space=pltpu.VMEM)
        hbm = pl.BlockSpec(memory_space=pl.ANY)
        bf16, f32 = jnp.bfloat16, jnp.float32
        message = lambda: pltpu.VMEM((experts, n, rows, half), bf16)
        y = pl.pallas_call(
            functools.partial(kernel, n, slots, experts),
            name="moe",
            out_shape=jax.ShapeDtypeStruct((tokens, dim), bf16),
            in_specs=[vmem, vmem] + [hbm] * 4,
            out_specs=vmem,
            scratch_shapes=[
                pltpu.VMEM((2 * tokens, half), bf16),
                message(), message(), message(), message(),
                pltpu.VMEM((n * slots, dim), bf16),
                pltpu.VMEM((n * slots, dim), f32),
                pltpu.VMEM((2 * tokens, half), f32),
                pltpu.VMEM((2, n * slots, TILE), bf16),
                pltpu.VMEM((top, 2 * tokens, 128), jnp.int32),
                pltpu.VMEM((top, 2 * tokens, 128), f32),
                pltpu.VMEM((RING, dim, TILE), bf16),
                pltpu.VMEM((RING, dim, TILE), bf16),
                pltpu.VMEM((RING, TILE, dim), bf16),
                pltpu.SemaphoreType.DMA((2,)),
                pltpu.SemaphoreType.DMA((3, RING)),
                pltpu.SemaphoreType.DMA((2 * experts, n - 1)),
                pltpu.SemaphoreType.DMA((2 * experts, n - 1)),
            ],
            compiler_params=pltpu.CompilerParams(
                collective_id=0, has_side_effects=True, vmem_limit_bytes=67_043_328),
        )(flat, gate, x.reshape(tokens, dim), w_gate, w_up, w_down)
        return y.reshape(x.shape)

    spread, held = P("dp", "ep"), P("ep")
    return jax.shard_map(
        step, mesh=mesh, in_specs=(spread,) * 4 + (held,) * 3, out_specs=spread, check_vma=False)
```

time: 226 us -> 121 us (0.54)
  Pallas kernels: 0 us -> 116 us
  matrix products: 84.2 us -> 0 us
  blocking collectives: 65.5 us -> 0 us
  waiting for transfers between devices: 49.1 us -> 0 us
  local copies, waits for them, and re-layouts: 22.2 us -> 2.16 us
  starting transfers between devices: 4.28 us -> 0 us
  other arithmetic: 0.01 us -> 2.64 us
    pallas_call x0 -> x1, Pallas kernels: none -> 116 us  [step(): pl.pallas_call(functools.partial(kernel, n, slots, experts), name='moe',...]
    dot_general x7 -> x0, matrix products: 84.2 us -> none  [einsum(): return jnp.einsum(form, a.astype(jnp.float32), b.astype(jnp.float32))]
    another operation x1 -> x0, blocking collectives: 65.5 us -> none  [placed(): return lax.with_sharding_constraint(v, NamedSharding(mesh, P(*spec)))]
    another operation x1 -> x0, waiting for transfers between devices: 49.1 us -> none  [placed(): return lax.with_sharding_constraint(v, NamedSharding(mesh, P(*spec)))]
    another operation x4 -> x0, local copies, waits for them, and re-layouts: 14.8 us -> none  [placed(): return lax.with_sharding_constraint(v, NamedSharding(mesh, P(*spec)))]
    unnamed x17 -> x1, local copies, waits for them, and re-layouts: 7.26 us -> 2.16 us
    another operation x1 -> x0, starting transfers between devices: 4.28 us -> none  [placed(): return lax.with_sharding_constraint(v, NamedSharding(mesh, P(*spec)))]
  transfers between devices with their start and end apart: 1 -> 0, of which waited for: 1 -> 0; matrix products, arithmetic and copies ran while one was open for 2% -> 0% of each run, Pallas kernels for 0% -> 0%
where the time goes in v1:
time: 121 us
  Pallas kernels  116 us (96%)
  other arithmetic  2.64 us (2%)
  local copies, waits for them, and re-layouts  2.16 us (2%)
    pallas_call x1, Pallas kernels, step(): pl.pallas_call(functools.partial(kernel, n, slots, experts), name='moe',...  116 us

profile of v1, /device:TPU:21, one launch (start us, length us, event | category | flops | bytes accessed | tf_op | source)
XLA Modules:
  0.0 120.9 jit_solution(16096194062633406773)
XLA Ops:
  0.0 1.3 %pad_maximum_fusion.gate_ref = f32[2,512]{1,0:T(2,128)} fusion(f32[2,256]{1,0:T(2,128)} %bitcast.12), kind=kLoop, calls=%fused_computation.1 | loop fusion | flops 1024 | bytes 6144 | tf_op jit(solution)/shard_map/concatenate | solution.py:253
  1.3 0.7 broadcast_add_fusion
  2.0 0.6 pad_add_fusion.flat_ref
  2.6 116.1 %moe.1 = bf16[256,1792]{1,0:T(8,128)(2,1)} custom-call(s32[2,512]{1,0:T(2,128)} %pad_add_fusion.flat_ref, f32[2,512]{1,0:T(2,128)} %pad_maximum_fusion.gate_ref, bf16[256,1792]{1,0:T(8,128)(2,1)} %bitcast.11, bf16[2,1792,4864]{2,1,0:T(8,128)(2,1)} %wg_hbm.1, bf16[2,1792,4864]{2,1,0:T(8,128)(2,1)} %wu_hbm.1, bf16[2,4864,1792]{2,1,0:T(8,128)(2,1)} %wd_hbm.1), custom_call_target="tpu_custom_call" | custom-call | tf_op jit(solution)/shard_map/moe/pallas_call | solution.py:258
  118.7 2.2 %copy.9 = bf16[1,1,256,1792]{3,2,1,0:T(8,128)(2,1)} copy(bf16[1,1,256,1792]{3,2,1,0:T(8,128)(2,1)} %bitcast.10) | data formatting | bytes 1835008

commit v2 on v1

--- a/solution.py
+++ b/solution.py
@@ -9,7 +9,7 @@
 
 CORES = 2
 TILE = 256
-RING = 16
+RING = 14
 GROUP = 4
 FAR = 1 << 16
 
@@ -20,18 +20,14 @@
 
 def offsets(n):
     chips = n // CORES
-    out = []
-    for far in range(chips // 2, 0, -1):
-        for way in (1, -1):
-            if way == -1 and 2 * far == chips:
-                continue
-            for core in range(CORES):
-                out.append(((way * far) % chips, core))
+    reach = range((chips - 1) // 2, 0, -1)
+    out = [(ahead, core) for far in reach for core in range(CORES) for ahead in (far, chips - far)]
+    out[2 * CORES:2 * CORES] = [(chips // 2, core) for core in range(CORES)]
     return out + [(0, core) for core in range(CORES - 1, -1, -1)]
 
 
-def kernel(n, slots, experts, flat_ref, gate_ref, x_hbm, wg_hbm, wu_hbm, wd_hbm, y_ref,
-           xs, zsend, zrecv, osend, orecv, z, acc, yacc, hid, cols, gcols, wg, wu, wd,
+def kernel(n, slots, experts, expert_hbm, slot_hbm, gate_hbm, x_hbm, wg_hbm, wu_hbm, wd_hbm, y_ref,
+           eidx, sidx, gates, xs, zsend, zrecv, osend, orecv, z, acc, yacc, hid, cols, gcols, wg, wu, wd,
            xsem, wsem, ssem, rsem):
     plan = offsets(n)
     self_at = n - 1
@@ -41,6 +37,7 @@
     dim = x_hbm.shape[1]
     half = dim // 2
     tokens = x_hbm.shape[0]
+    top = expert_hbm.shape[0]
     rows = 2 * slots
     tiles = wd_hbm.shape[1] // TILE
     total = experts * tiles
@@ -69,19 +66,21 @@
     out_copy = lambda e, i: remote(e, e, i, zsend, zrecv, False)
     back_copy = lambda e, i: remote(experts + e, e, i, osend, orecv, True)
 
-    xcopies = [pltpu.make_async_copy(x_hbm.at[:, pl.ds(k * half, half)], xs.at[pl.ds(k * tokens, tokens), :], xsem.at[k])
-               for k in range(2)]
-    for c in xcopies:
+    small = [pltpu.make_async_copy(src, dst, xsem.at[2 + k])
+             for k, (src, dst) in enumerate(((expert_hbm, eidx), (slot_hbm, sidx), (gate_hbm, gates)))]
+    halves = [pltpu.make_async_copy(x_hbm.at[:, pl.ds(k * half, half)], xs.at[pl.ds(k * tokens, tokens), :], xsem.at[k])
+              for k in range(2)]
+    for c in small + halves:
         c.start()
 
     barrier = pltpu.get_barrier_semaphore()
     for k in range(1, n):
         pl.semaphore_signal(barrier, inc=1, device_id={"ep": lax.rem(me + k, n)}, device_id_type=pl.DeviceIdType.MESH)
 
-    @pl.loop(0, ring)
-    def _(q):
-        for which in range(3):
-            weight_copy(q, which).start()
+    for c in small:
+        c.wait()
+    line = jnp.where(sidx[...] < slots, eidx[...] * slots + sidx[...], -1)
+    line = jnp.concatenate([line, line + FAR], axis=1)
 
     def wanted(e, g, shape, axis):
         at = lax.broadcasted_iota(jnp.int32, shape, axis)
@@ -95,7 +94,7 @@
 
     def dispatch(e, g):
         want = wanted(e, g, (GROUP * rows, 2 * tokens), 0)
-        hit = (flat_ref[0:1, :] == want) | (flat_ref[1:2, :] == want)
+        hit = functools.reduce(jnp.logical_or, [line[k:k + 1, :] == want for k in range(top)])
         mask = jnp.where(hit, 1.0, 0.0).astype(jnp.bfloat16)
         packed = dot(mask, xs[...]).astype(jnp.bfloat16)
         for j in range(GROUP):
@@ -107,19 +106,28 @@
                 zsend[e, i] = piece
 
     groups = n // GROUP
-    for c in xcopies:
-        c.wait()
     for g in range(groups):
+        if g == 0:
+            for c in halves:
+                c.wait()
         dispatch(0, g)
-    pl.semaphore_wait(barrier, n - 1)
-    for i in range(self_at):
-        out_copy(0, i).start()
+        if g == 0:
+            pl.semaphore_wait(barrier, n - 1)
+        for i in range(g * GROUP, min((g + 1) * GROUP, self_at)):
+            out_copy(0, i).start()
+
+    @pl.loop(0, ring)
+    def _(q):
+        for which in range(3):
+            weight_copy(q, which).start()
+
     for g in range(groups):
         dispatch(1, g)
-    for k in range(2):
-        cols[k] = jnp.broadcast_to(flat_ref[k:k + 1, :], (128, 2 * tokens)).T
-        rounded = gate_ref[k:k + 1, :].astype(jnp.bfloat16).astype(jnp.float32)
-        gcols[k] = jnp.broadcast_to(rounded, (128, 2 * tokens)).T
+    rounded = gates[...].astype(jnp.bfloat16).astype(jnp.float32)
+    rounded = jnp.concatenate([rounded, rounded], axis=1)
+    for k in range(top):
+        cols[k] = jnp.broadcast_to(line[k:k + 1, :], (128, 2 * tokens)).T
+        gcols[k] = jnp.broadcast_to(rounded[k:k + 1, :], (128, 2 * tokens)).T
     for i in range(self_at):
         out_copy(0, i).wait_send()
         out_copy(1, i).start()
@@ -211,7 +219,7 @@
         for g in range(groups):
             want = wanted(e, g, shape, 1)
             weight = jnp.zeros(shape, jnp.float32)
-            for k in range(2):
+            for k in range(top):
                 weight += jnp.where(cols[k, :, 0:1] == want, gcols[k, :, 0:1], 0.0)
             weight = weight.astype(jnp.bfloat16)
             for j in range(GROUP):
@@ -221,6 +229,10 @@
             term = dot(weight, orecv[e, g * GROUP:(g + 1) * GROUP].reshape(GROUP * rows, half))
             if e == 0 and g == 0:
                 yacc[...] = term
+            elif e == experts - 1 and g == groups - 1:
+                for k in range(2):
+                    at = slice(k * tokens, (k + 1) * tokens)
+                    y_ref[:, k * half:(k + 1) * half] = (yacc[at, :] + term[at]).astype(jnp.bfloat16)
             else:
                 yacc[...] += term
 
@@ -230,13 +242,10 @@
         give_back(e)
     for e in range(experts):
         combine(e)
-    for k in range(2):
-        y_ref[:, k * half:(k + 1) * half] = yacc[k * tokens:(k + 1) * tokens, :].astype(jnp.bfloat16)
     for i in range(self_at):
         out_copy(1, i).wait_send()
         for e in range(experts):
             back_copy(e, i).wait_send()
-
 
 def solution(mesh):
     n = mesh.shape["ep"]
@@ -248,20 +257,19 @@
         slots = 5 * tokens * top // (4 * experts * n)
         rows, half = 2 * slots, dim // 2
         expert, slot, gate = (v.reshape(tokens, top).T for v in (expert, slot, gate))
-        flat = jnp.where(slot < slots, expert * slots + slot, -1)
-        flat = jnp.concatenate([flat, flat + FAR], axis=1)
-        gate = jnp.concatenate([gate, gate], axis=1)
-        vmem = pl.BlockSpec(memory_space=pltpu.VMEM)
         hbm = pl.BlockSpec(memory_space=pl.ANY)
         bf16, f32 = jnp.bfloat16, jnp.float32
         message = lambda: pltpu.VMEM((experts, n, rows, half), bf16)
         y = pl.pallas_call(
             functools.partial(kernel, n, slots, experts),
             name="moe",
-            out_shape=jax.ShapeDtypeStruct((tokens, dim), bf16),
-            in_specs=[vmem, vmem] + [hbm] * 4,
-            out_specs=vmem,
+            out_shape=pltpu.VMEM((tokens, dim), bf16),
+            in_specs=[hbm] * 7,
+            out_specs=pl.BlockSpec(memory_space=pltpu.VMEM),
             scratch_shapes=[
+                pltpu.VMEM((top, tokens), jnp.int32),
+                pltpu.VMEM((top, tokens), jnp.int32),
+                pltpu.VMEM((top, tokens), f32),
                 pltpu.VMEM((2 * tokens, half), bf16),
                 message(), message(), message(), message(),
                 pltpu.VMEM((n * slots, dim), bf16),
@@ -273,14 +281,14 @@
                 pltpu.VMEM((RING, dim, TILE), bf16),
                 pltpu.VMEM((RING, dim, TILE), bf16),
                 pltpu.VMEM((RING, TILE, dim), bf16),
-                pltpu.SemaphoreType.DMA((2,)),
+                pltpu.SemaphoreType.DMA((5,)),
                 pltpu.SemaphoreType.DMA((3, RING)),
                 pltpu.SemaphoreType.DMA((2 * experts, n - 1)),
                 pltpu.SemaphoreType.DMA((2 * experts, n - 1)),
             ],
             compiler_params=pltpu.CompilerParams(
-                collective_id=0, has_side_effects=True, vmem_limit_bytes=67_043_328),
-        )(flat, gate, x.reshape(tokens, dim), w_gate, w_up, w_down)
+                collective_id=0, has_side_effects=True, vmem_limit_bytes=62_500_000),
+        )(expert, slot, gate, x.reshape(tokens, dim), w_gate, w_up, w_down)
         return y.reshape(x.shape)
 
     spread, held = P("dp", "ep"), P("ep")

time: 121 us -> 114 us (0.942)
  Pallas kernels: 116 us -> 113 us
  other arithmetic: 2.64 us -> 0 us
  local copies, waits for them, and re-layouts: 2.16 us -> 0.93 us
    pallas_call x1, Pallas kernels: 116 us -> 113 us  [step(): pl.pallas_call(functools.partial(kernel, n, slots, experts), name='moe',...]
    concatenate x2 -> x0, other arithmetic: 1.94 us -> none  [the longest x1 1.34 us: step(): gate = jnp.concatenate([gate, gate], axis=1)]
    unnamed x1, local copies, waits for them, and re-layouts: 2.16 us -> 0.93 us
where the time goes in v2:
time: 114 us
  Pallas kernels  113 us (99%)
    pallas_call x1, Pallas kernels, step(): pl.pallas_call(functools.partial(kernel, n, slots, experts), name='moe',...  113 us

profile of v2, /device:TPU:21, one launch (start us, length us, event | category | flops | bytes accessed | tf_op | source)
XLA Modules:
  0.0 114.0 jit_solution(15916327409409886787)
XLA Ops:
  0.0 113.1 %moe.1 = bf16[256,1792]{1,0:T(8,128)(2,1)S(1)} custom-call(s32[2,256]{1,0:T(2,128)} %bitcast.13, s32[2,256]{1,0:T(2,128)} %bitcast.14, f32[2,256]{1,0:T(2,128)} %bitcast.15, bf16[256,1792]{1,0:T(8,128)(2,1)} %bitcast.12, bf16[2,1792,4864]{2,1,0:T(8,128)(2,1)} %wg_hbm.1, bf16[2,1792,4864]{2,1,0:T(8,128)(2,1)} %wu_hbm.1, bf16[2,4864,1792]{2,1,0:T(8,128)(2,1)} %wd_hbm.1), custom_call_target="tpu_custom_call" | custom-call | tf_op jit(solution)/shard_map/moe/pallas_call | solution.py:263
  113.1 0.9 copy.9

commit v3 on v2

--- a/solution.py
+++ b/solution.py
@@ -20,15 +20,22 @@
 
 def offsets(n):
     chips = n // CORES
-    reach = range((chips - 1) // 2, 0, -1)
-    out = [(ahead, core) for far in reach for core in range(CORES) for ahead in (far, chips - far)]
-    out[2 * CORES:2 * CORES] = [(chips // 2, core) for core in range(CORES)]
+    both = lambda far: [(ahead, core) for core in range(CORES) for ahead in (far, chips - far)]
+    reach = range((chips - 1) // 2, 1, -1)
+    out = both(1) + [p for far in reach for p in both(far)]
+    out[4 * CORES:4 * CORES] = [(chips // 2, core) for core in range(CORES)]
     return out + [(0, core) for core in range(CORES - 1, -1, -1)]
+
+
+def near(n):
+    chips = n // CORES
+    step = (chips // 2 + 1) // 2
+    return [(ahead % chips, core) for ahead in range(-step, step + 1) for core in range(CORES) if (ahead, core) != (0, 0)]
 
 
 def kernel(n, slots, experts, expert_hbm, slot_hbm, gate_hbm, x_hbm, wg_hbm, wu_hbm, wd_hbm, y_ref,
            eidx, sidx, gates, xs, zsend, zrecv, osend, orecv, z, acc, yacc, hid, cols, gcols, wg, wu, wd,
-           xsem, wsem, ssem, rsem):
+           xsem, wsem, ssem, rsem, known):
     plan = offsets(n)
     self_at = n - 1
     chips = n // CORES
@@ -45,7 +52,13 @@
 
     def partner(i, back):
         ahead, other = plan[i]
-        ahead = (chips - ahead) % chips if back else ahead
+        return device((chips - ahead) % chips if back else ahead, other)
+
+    def greet(sem):
+        for there in near(n):
+            pl.semaphore_signal(sem, inc=1, device_id={"ep": device(*there)}, device_id_type=pl.DeviceIdType.MESH)
+
+    def device(ahead, other):
         return lax.rem(chip + ahead, chips) * CORES + lax.rem(core + other, CORES)
 
     def weight_copy(q, which):
@@ -74,8 +87,7 @@
         c.start()
 
     barrier = pltpu.get_barrier_semaphore()
-    for k in range(1, n):
-        pl.semaphore_signal(barrier, inc=1, device_id={"ep": lax.rem(me + k, n)}, device_id_type=pl.DeviceIdType.MESH)
+    greet(barrier)
 
     for c in small:
         c.wait()
@@ -112,7 +124,10 @@
                 c.wait()
         dispatch(0, g)
         if g == 0:
-            pl.semaphore_wait(barrier, n - 1)
+            pl.semaphore_wait(barrier, len(near(n)))
+            greet(known)
+        if g == 1:
+            pl.semaphore_wait(known, len(near(n)))
         for i in range(g * GROUP, min((g + 1) * GROUP, self_at)):
             out_copy(0, i).start()
 
@@ -192,10 +207,12 @@
         acc[...] += dot(hid[(tiles - 1) % 2], wd[last % ring])
         refill(last, 2)
 
+    homeward = [*range(1, groups), 0]
+
     def give_back(e):
         shape = (GROUP * rows, quarter)
         there = lax.broadcasted_iota(jnp.int32, shape, 0)
-        for g in range(groups):
+        for g in homeward:
             done = acc[g * quarter:(g + 1) * quarter, :].astype(jnp.bfloat16)
             packed = jnp.zeros((GROUP * rows, half), jnp.float32)
             for k in range(2):
@@ -216,7 +233,7 @@
 
     def combine(e):
         shape = (2 * tokens, GROUP * rows)
-        for g in range(groups):
+        for g in homeward:
             want = wanted(e, g, shape, 1)
             weight = jnp.zeros(shape, jnp.float32)
             for k in range(top):
@@ -227,9 +244,9 @@
                 if i != self_at:
                     back_copy(e, i).wait_recv()
             term = dot(weight, orecv[e, g * GROUP:(g + 1) * GROUP].reshape(GROUP * rows, half))
-            if e == 0 and g == 0:
+            if e == 0 and g == homeward[0]:
                 yacc[...] = term
-            elif e == experts - 1 and g == groups - 1:
+            elif e == experts - 1 and g == homeward[-1]:
                 for k in range(2):
                     at = slice(k * tokens, (k + 1) * tokens)
                     y_ref[:, k * half:(k + 1) * half] = (yacc[at, :] + term[at]).astype(jnp.bfloat16)
@@ -285,6 +302,7 @@
                 pltpu.SemaphoreType.DMA((3, RING)),
                 pltpu.SemaphoreType.DMA((2 * experts, n - 1)),
                 pltpu.SemaphoreType.DMA((2 * experts, n - 1)),
+                pltpu.SemaphoreType.REGULAR,
             ],
             compiler_params=pltpu.CompilerParams(
                 collective_id=0, has_side_effects=True, vmem_limit_bytes=62_500_000),

time: 114 us -> 113 us (level)
  no operation moved by 1% of the time
where the time goes in v3:
time: 113 us
  Pallas kernels  112 us (99%)
    pallas_call x1, Pallas kernels, step(): pl.pallas_call(functools.partial(kernel, n, slots, experts), name='moe',...  112 us

profile of v3, /device:TPU:21, one launch (start us, length us, event | category | flops | bytes accessed | tf_op | source)
XLA Modules:
  0.0 112.9 jit_solution(13826911075576193117)
XLA Ops:
  0.0 111.9 %moe.1 = bf16[256,1792]{1,0:T(8,128)(2,1)S(1)} custom-call(s32[2,256]{1,0:T(2,128)} %bitcast.13, s32[2,256]{1,0:T(2,128)} %bitcast.14, f32[2,256]{1,0:T(2,128)} %bitcast.15, bf16[256,1792]{1,0:T(8,128)(2,1)} %bitcast.12, bf16[2,1792,4864]{2,1,0:T(8,128)(2,1)} %wg_hbm.1, bf16[2,1792,4864]{2,1,0:T(8,128)(2,1)} %wu_hbm.1, bf16[2,4864,1792]{2,1,0:T(8,128)(2,1)} %wd_hbm.1), custom_call_target="tpu_custom_call" | custom-call | tf_op jit(solution)/shard_map/moe/pallas_call | solution.py:280
  112.0 0.9 copy.9

commit v4 on v3

--- a/solution.py
+++ b/solution.py
@@ -83,11 +83,10 @@
              for k, (src, dst) in enumerate(((expert_hbm, eidx), (slot_hbm, sidx), (gate_hbm, gates)))]
     halves = [pltpu.make_async_copy(x_hbm.at[:, pl.ds(k * half, half)], xs.at[pl.ds(k * tokens, tokens), :], xsem.at[k])
               for k in range(2)]
+    barrier = pltpu.get_barrier_semaphore()
+    greet(barrier)
     for c in small + halves:
         c.start()
-
-    barrier = pltpu.get_barrier_semaphore()
-    greet(barrier)
 
     for c in small:
         c.wait()

time: 113 us -> 113 us (level)
  no operation moved by 1% of the time
where the time goes in v4:
time: 113 us
  Pallas kernels  112 us (99%)
    pallas_call x1, Pallas kernels, step(): pl.pallas_call(functools.partial(kernel, n, slots, experts), name='moe',...  112 us

profile of v4, /device:TPU:21, one launch (start us, length us, event | category | flops | bytes accessed | tf_op | source)
XLA Modules:
  0.0 112.7 jit_solution(2769262441220190398)
XLA Ops:
  0.0 111.8 %moe.1 = bf16[256,1792]{1,0:T(8,128)(2,1)S(1)} custom-call(s32[2,256]{1,0:T(2,128)} %bitcast.13, s32[2,256]{1,0:T(2,128)} %bitcast.14, f32[2,256]{1,0:T(2,128)} %bitcast.15, bf16[256,1792]{1,0:T(8,128)(2,1)} %bitcast.12, bf16[2,1792,4864]{2,1,0:T(8,128)(2,1)} %wg_hbm.1, bf16[2,1792,4864]{2,1,0:T(8,128)(2,1)} %wu_hbm.1, bf16[2,4864,1792]{2,1,0:T(8,128)(2,1)} %wd_hbm.1), custom_call_target="tpu_custom_call" | custom-call | tf_op jit(solution)/shard_map/moe/pallas_call | solution.py:279
  111.8 0.9 copy.9
